TPU v7x, 32 devices: a whole 2x2x4 slice. The times are simulated.
32 devices in a mesh: dp: 4 (over z), seq: 8 (over y, x, core).
Axes of the slice: x: 2, y: 2, z: 4, core: 2. Of those that a mesh axis runs over, the one named last changes fastest.
Arguments:
- queries: bfloat16 [4096, 64, 128], P(('dp', 'seq')), parts along dimension 0, may hold values from -52 to 52
- keys: bfloat16 [4096, 8, 128], P(('dp', 'seq')), parts along dimension 0, may hold values from -6 to 6
- values: bfloat16 [4096, 8, 128], P(('dp', 'seq')), parts along dimension 0, may hold values from -6 to 6
- doc_ids: int32 [4096], P(('dp', 'seq')), parts along dimension 0, may hold values from 0 to 7, never falling along the last dimension, each value on 1 to 512 neighbouring positions
- counts: int32 [32], P('dp'), parts along dimension 0, may hold values from 64 to 128
Outputs:
- attended: bfloat16 [4096, 64, 128], P(('dp', 'seq')), parts along dimension 0
There are 4 independent parts, one for each index of `dp`. A program takes and returns all parts, laid end to end along the dimension named above; each array names one. Nothing has to cross between parts.
Inputs may be any that keep to these rules, and one draw needn't show every extreme that they name: `doc_ids`: document numbers never fall along the sequence; each document has 1 to 512 positions. The first counts[j] positions of shard j are real tokens, the others padding.
All inputs are finite; a program needn't handle non-finite values.
Results may differ from a plain program's by a relative error of at most 0.003.
Values may be sent and summed in bfloat16 or wider, within the bound.
A program may use at most 64 MiB of HBM per device.

v0:
```python
import math

import jax
import jax.numpy as jnp
from jax import lax
from jax.sharding import PartitionSpec as P

DOC_MOST = 512


def from_behind(array, axis, by):
    size = lax.axis_size(axis)
    pairs = [(i, i + by) for i in range(size) if 0 <= i + by < size]
    return lax.ppermute(array, axis, pairs)


def window_attend(queries, keys, values, all_docs, live_rows, device, shard_rows):
    reach = (DOC_MOST + shard_rows - 1) // shard_rows
    head_size = queries.shape[2]
    kv_heads_all = keys.shape[1]
    queries_per_group = queries.shape[1] // kv_heads_all
    score_scale = 1.0 / math.sqrt(head_size)
    key_parts = []
    value_parts = []
    for offset in range(reach, 0, -1):
        earlier_keys, earlier_values = from_behind((keys, values), "seq", offset)
        key_parts.append(earlier_keys)
        value_parts.append(earlier_values)
    window_keys = jnp.concatenate(key_parts + [keys], axis=0)
    window_values = jnp.concatenate(value_parts + [values], axis=0)
    window_rows = window_keys.shape[0]
    own_start = device * shard_rows
    window_start = own_start - reach * shard_rows
    padded_docs = jnp.concatenate([jnp.full((reach * shard_rows,), -1, jnp.int32), all_docs])
    padded_live = jnp.concatenate([jnp.zeros((reach * shard_rows,), jnp.bool_), live_rows])
    key_doc = lax.dynamic_slice_in_dim(padded_docs, own_start, window_rows, 0)
    key_live = lax.dynamic_slice_in_dim(padded_live, own_start, window_rows, 0)
    key_pos = window_start + jnp.arange(window_rows, dtype=jnp.int32)
    query_pos = own_start + jnp.arange(shard_rows, dtype=jnp.int32)
    query_doc = lax.dynamic_slice_in_dim(all_docs, own_start, shard_rows, 0)
    query_live = lax.dynamic_slice_in_dim(live_rows, own_start, shard_rows, 0)
    allowed = (
        (key_doc[None, :] == query_doc[:, None])
        & (key_pos[None, :] <= query_pos[:, None])
        & key_live[None, :]
        & (key_pos[None, :] >= 0)
    )
    grouped_queries = jnp.transpose(
        queries.reshape(shard_rows, kv_heads_all, queries_per_group, head_size), (1, 0, 2, 3)
    )
    grouped_keys = jnp.transpose(window_keys, (1, 0, 2))
    grouped_values = jnp.transpose(window_values, (1, 0, 2))

    def one_group(operands):
        query_group, key_group, value_group = operands
        scores = (
            jnp.einsum("qgd,kd->gqk", query_group, key_group, preferred_element_type=jnp.float32)
            * score_scale
        )
        masked = jnp.where(allowed[None], scores, -1e30)
        top = jnp.max(masked, axis=-1, keepdims=True)
        weights = jnp.where(allowed[None], jnp.exp(scores - top), 0.0)
        norm_sum = jnp.sum(weights, axis=-1)
        mixed = jnp.einsum(
            "gqk,kd->qgd",
            weights.astype(jnp.bfloat16),
            value_group,
            preferred_element_type=jnp.float32,
        )
        norm_rows = jnp.transpose(norm_sum, (1, 0))[:, :, None]
        norm_rows = jnp.where(query_live[:, None, None], norm_rows, 1.0)
        return jnp.where(query_live[:, None, None], mixed / norm_rows, 0.0).astype(jnp.bfloat16)

    outputs = lax.map(one_group, (grouped_queries, grouped_keys, grouped_values))
    return jnp.transpose(outputs, (1, 0, 2, 3)).reshape(
        shard_rows, kv_heads_all * queries_per_group, head_size
    )


def local(queries, keys, values, doc_ids, counts):
    shard_count = lax.axis_size("seq")
    shard_rows = queries.shape[0]
    row_count = shard_rows * shard_count
    device = lax.axis_index("seq")
    all_docs = lax.all_gather(doc_ids, "seq", axis=0, tiled=True)
    positions = jnp.arange(row_count, dtype=jnp.int32)
    live_rows = positions % shard_rows < jnp.repeat(
        counts, shard_rows, total_repeat_length=row_count
    )
    return window_attend(queries, keys, values, all_docs, live_rows, device, shard_rows)


def solution(mesh):
    in_specs = (
        P(("dp", "seq"), None, None),
        P(("dp", "seq"), None, None),
        P(("dp", "seq"), None, None),
        P(("dp", "seq")),
        P("dp"),
    )
    out_specs = P(("dp", "seq"), None, None)
    return jax.shard_map(local, mesh=mesh, in_specs=in_specs, out_specs=out_specs, check_vma=False)
```

profile of v0, /device:TPU:1, one launch (start us, length us, event | category | flops | bytes accessed | tf_op | source)
XLA Modules:
  0.0 111.8 jit_solution(1932773855371573)
XLA Ops:
  1.2 4.7 %collective-permute-start = (bf16[128,8,128]{0,2,1:T(8,128)(2,1)S(1)}, bf16[128,8,128]{0,2,1:T(8,128)(2,1)}, u32[]{:S(2)}, u32[]{:S(2)}) collective-permute-start(bf16[128,8,128]{0,2,1:T(8,128)(2,1)S(1)} %copy.20), channel_id=1, source_target_pairs={{0,4},{1,5},{2,6},{3,7},{8,12},{9,13},{10,14},{11,15},{16,20},{17,... | collective-permute-start | bytes 786440 | tf_op jit(solution)/shard_map/ppermute | solution.py:14
  7.8 3.1 %collective-permute-start.2 = (bf16[128,8,128]{0,2,1:T(8,128)(2,1)S(1)}, bf16[128,8,128]{0,2,1:T(8,128)(2,1)S(1)}, u32[]{:S(2)}, u32[]{:S(2)}) collective-permute-start(bf16[128,8,128]{0,2,1:T(8,128)(2,1)S(1)} %copy.20), channel_id=1, source_target_pairs={{0,2},{1,3},{2,4},{3,5},{4,6},{5,7},{8,10},{9,11},{10,12},{11,13},... | collective-permute-start | bytes 786440 | tf_op jit(solution)/shard_map/ppermute | solution.py:14
  10.9 2.8 %collective-permute-start.3 = (bf16[128,8,128]{0,2,1:T(8,128)(2,1)S(1)}, bf16[128,8,128]{0,2,1:T(8,128)(2,1)S(1)}, u32[]{:S(2)}, u32[]{:S(2)}) collective-permute-start(bf16[128,8,128]{0,2,1:T(8,128)(2,1)S(1)} %copy.20), channel_id=1, source_target_pairs={{0,1},{1,2},{2,3},{3,4},{4,5},{5,6},{6,7},{8,9},{9,10},{10,11},{11... | collective-permute-start | bytes 786440 | tf_op jit(solution)/shard_map/ppermute | solution.py:14
  17.7 16.1 %all-gather = s32[8,1,128]{2,1,0:T(1,128)S(1)} all-gather(s32[1,1,128]{2,1,0:T(1,128)} %bitcast.154), channel_id=1, replica_groups=mesh['dp'=4,'seq'=8] {'seq'}, dimensions={0}, use_global_device_ids=true | all-gather | bytes 4608 | tf_op jit(solution)/shard_map/all_gather | solution.py:85
  33.8 4.6 %compare_select_fusion.1 = s32[1024,1]{0,1:T(1,128)S(1)} fusion(s32[]{:T(128)} %bitcast.5, s32[]{:T(128)} %bitcast.6, s32[]{:T(128)} %bitcast.7, s32[]{:T(128)} %bitcast.8, s32[]{:T(128)} %bitcast.9, s32[]{:T(128)} %bitcast.11, s32[]{:T(128)} %bitcast.10, s32[1024,1]{0,1:T(1,128)S(1)} %bitcast.150, s32[1024,1]{0,1:T(1,128)S(1)} %bitcast.148), kind=kLoop, calls=%fused_computation.54 | loop fusion | flops 14336 | bytes 12316 | tf_op jit(solution)/shard_map/jit(_take)/gather | solution.py:87
  39.4 2.9 %copy.30 = bf16[128,64,128]{2,0,1:T(8,128)(2,1)S(1)} copy(bf16[128,64,128]{2,1,0:T(8,128)(2,1)} %param.9) | data formatting | bytes 4194304 | tf_op args[0]
  42.4 2.9 %collective-permute-start.5 = (bf16[128,8,128]{2,0,1:T(8,128)(2,1)S(1)}, bf16[128,8,128]{2,0,1:T(8,128)(2,1)S(1)}, u32[]{:S(2)}, u32[]{:S(2)}) collective-permute-start(bf16[128,8,128]{2,0,1:T(8,128)(2,1)S(1)} %copy.25), channel_id=1, source_target_pairs={{0,3},{1,4},{2,5},{3,6},{4,7},{8,11},{9,12},{10,13},{11,14},{12,15... | collective-permute-start | bytes 786440 | tf_op jit(solution)/shard_map/ppermute | solution.py:14
  46.4 3.6 %collective-permute-start.6 = (bf16[128,8,128]{2,0,1:T(8,128)(2,1)S(1)}, bf16[128,8,128]{2,0,1:T(8,128)(2,1)S(1)}, u32[]{:S(2)}, u32[]{:S(2)}) collective-permute-start(bf16[128,8,128]{2,0,1:T(8,128)(2,1)S(1)} %copy.25), channel_id=1, source_target_pairs={{0,2},{1,3},{2,4},{3,5},{4,6},{5,7},{8,10},{9,11},{10,12},{11,13},... | collective-permute-start | bytes 786440 | tf_op jit(solution)/shard_map/ppermute | solution.py:14
  51.0 3.4 %collective-permute-start.7 = (bf16[128,8,128]{2,0,1:T(8,128)(2,1)S(1)}, bf16[128,8,128]{2,0,1:T(8,128)(2,1)S(1)}, u32[]{:S(2)}, u32[]{:S(2)}) collective-permute-start(bf16[128,8,128]{2,0,1:T(8,128)(2,1)S(1)} %copy.25), channel_id=1, source_target_pairs={{0,1},{1,2},{2,3},{3,4},{4,5},{5,6},{6,7},{8,9},{9,10},{10,11},{11... | collective-permute-start | bytes 786440 | tf_op jit(solution)/shard_map/ppermute | solution.py:14
  54.7 5.1 %collective-permute-done.5 = bf16[128,8,128]{2,0,1:T(8,128)(2,1)S(1)} collective-permute-done((bf16[128,8,128]{2,0,1:T(8,128)(2,1)S(1)}, bf16[128,8,128]{2,0,1:T(8,128)(2,1)S(1)}, u32[]{:S(2)}, u32[]{:S(2)}) %collective-permute-start.5) | collective-permute-done | bytes 262176 | tf_op jit(solution)/shard_map/ppermute | solution.py:14
  61.1 46.5 %while.12 = (s32[]{:T(128)}, bf16[8,128,8,128]{1,3,2,0:T(8,128)(2,1)}, pred[128]{0:T(512)(128)(4,1)S(1)}, bf16[8,640,128]{1,2,0:T(8,128)(2,1)}, bf16[8,640,128]{...) while((s32[]{:T(128)}, ...), condition=%wide.region_3.4_spmd.clone, body=%wide.region_0.3_spmd.clone.sunk | while | flops 847531264 | bytes 2569213 | solution.py:74
  63.9 3.0 %fusion.130 = bf16[8,128,8,128]{1,3,2,0:T(8,128)(2,1)} fusion(bf16[8,128,8,128]{1,3,2,0:T(8,128)(2,1)} %get-tuple-element.208, s32[]{:T(128)} %get-tuple-element.207, f32[128,8]{0,1:T(8,128)S(1)} %select_bitcast_fusion.2, pred[128]{0:T(512)(128)(4,1)S(1)} %get-tuple-element.222, bf16[8,640,128]{1,2,0:T(8,128)(2,1)} %get-tuple-element.223, ...), kind=kOutput, calls=%fused_computation.18.clone.1 | convolution fusion | flops 507643520 | bytes 1449472 | tf_op jit(solution)/shard_map/while/body/eval_jaxpr/gqk,kd->qgd/dot_general | solution.py:64
  69.7 3.0 %fusion.130 = bf16[8,128,8,128]{1,3,2,0:T(8,128)(2,1)} fusion(bf16[8,128,8,128]{1,3,2,0:T(8,128)(2,1)} %get-tuple-element.208, s32[]{:T(128)} %get-tuple-element.207, f32[128,8]{0,1:T(8,128)S(1)} %select_bitcast_fusion.2, pred[128]{0:T(512)(128)(4,1)S(1)} %get-tuple-element.222, bf16[8,640,128]{1,2,0:T(8,128)(2,1)} %get-tuple-element.223, ...), kind=kOutput, calls=%fused_computation.18.clone.1 | convolution fusion | flops 507643520 | bytes 1449472 | tf_op jit(solution)/shard_map/while/body/eval_jaxpr/gqk,kd->qgd/dot_general | solution.py:64
  73.5 2.1 %fusion.129 = f32[8,128]{1,0:T(8,128)S(1)} fusion(pred[128,640]{0,1:T(8,128)(4,1)S(1)} %and_and_fusion.2, bf16[8,128,8,128]{3,1,2,0:T(8,128)(2,1)S(1)} %get-tuple-element.225, s32[]{:T(128)} %get-tuple-element.207, bf16[8,640,128]{2,1,0:T(8,128)(2,1)} %get-tuple-element.224), kind=kOutput, calls=%fused_computation.76.clone.1 | convolution fusion | flops 339477120 | bytes 1021952 | tf_op jit(solution)/shard_map/while/body/eval_jaxpr/sub | solution.py:62
  75.6 3.0 %fusion.130 = bf16[8,128,8,128]{1,3,2,0:T(8,128)(2,1)} fusion(bf16[8,128,8,128]{1,3,2,0:T(8,128)(2,1)} %get-tuple-element.208, s32[]{:T(128)} %get-tuple-element.207, f32[128,8]{0,1:T(8,128)S(1)} %select_bitcast_fusion.2, pred[128]{0:T(512)(128)(4,1)S(1)} %get-tuple-element.222, bf16[8,640,128]{1,2,0:T(8,128)(2,1)} %get-tuple-element.223, ...), kind=kOutput, calls=%fused_computation.18.clone.1 | convolution fusion | flops 507643520 | bytes 1449472 | tf_op jit(solution)/shard_map/while/body/eval_jaxpr/gqk,kd->qgd/dot_general | solution.py:64
  79.3 2.1 %fusion.129 = f32[8,128]{1,0:T(8,128)S(1)} fusion(pred[128,640]{0,1:T(8,128)(4,1)S(1)} %and_and_fusion.2, bf16[8,128,8,128]{3,1,2,0:T(8,128)(2,1)S(1)} %get-tuple-element.225, s32[]{:T(128)} %get-tuple-element.207, bf16[8,640,128]{2,1,0:T(8,128)(2,1)} %get-tuple-element.224), kind=kOutput, calls=%fused_computation.76.clone.1 | convolution fusion | flops 339477120 | bytes 1021952 | tf_op jit(solution)/shard_map/while/body/eval_jaxpr/sub | solution.py:62
  81.4 3.0 %fusion.130 = bf16[8,128,8,128]{1,3,2,0:T(8,128)(2,1)} fusion(bf16[8,128,8,128]{1,3,2,0:T(8,128)(2,1)} %get-tuple-element.208, s32[]{:T(128)} %get-tuple-element.207, f32[128,8]{0,1:T(8,128)S(1)} %select_bitcast_fusion.2, pred[128]{0:T(512)(128)(4,1)S(1)} %get-tuple-element.222, bf16[8,640,128]{1,2,0:T(8,128)(2,1)} %get-tuple-element.223, ...), kind=kOutput, calls=%fused_computation.18.clone.1 | convolution fusion | flops 507643520 | bytes 1449472 | tf_op jit(solution)/shard_map/while/body/eval_jaxpr/gqk,kd->qgd/dot_general | solution.py:64
  87.2 3.0 %fusion.130 = bf16[8,128,8,128]{1,3,2,0:T(8,128)(2,1)} fusion(bf16[8,128,8,128]{1,3,2,0:T(8,128)(2,1)} %get-tuple-element.208, s32[]{:T(128)} %get-tuple-element.207, f32[128,8]{0,1:T(8,128)S(1)} %select_bitcast_fusion.2, pred[128]{0:T(512)(128)(4,1)S(1)} %get-tuple-element.222, bf16[8,640,128]{1,2,0:T(8,128)(2,1)} %get-tuple-element.223, ...), kind=kOutput, calls=%fused_computation.18.clone.1 | convolution fusion | flops 507643520 | bytes 1449472 | tf_op jit(solution)/shard_map/while/body/eval_jaxpr/gqk,kd->qgd/dot_general | solution.py:64
  93.0 3.0 %fusion.130 = bf16[8,128,8,128]{1,3,2,0:T(8,128)(2,1)} fusion(bf16[8,128,8,128]{1,3,2,0:T(8,128)(2,1)} %get-tuple-element.208, s32[]{:T(128)} %get-tuple-element.207, f32[128,8]{0,1:T(8,128)S(1)} %select_bitcast_fusion.2, pred[128]{0:T(512)(128)(4,1)S(1)} %get-tuple-element.222, bf16[8,640,128]{1,2,0:T(8,128)(2,1)} %get-tuple-element.223, ...), kind=kOutput, calls=%fused_computation.18.clone.1 | convolution fusion | flops 507643520 | bytes 1449472 | tf_op jit(solution)/shard_map/while/body/eval_jaxpr/gqk,kd->qgd/dot_general | solution.py:64
  96.8 2.1 %fusion.129 = f32[8,128]{1,0:T(8,128)S(1)} fusion(pred[128,640]{0,1:T(8,128)(4,1)S(1)} %and_and_fusion.2, bf16[8,128,8,128]{3,1,2,0:T(8,128)(2,1)S(1)} %get-tuple-element.225, s32[]{:T(128)} %get-tuple-element.207, bf16[8,640,128]{2,1,0:T(8,128)(2,1)} %get-tuple-element.224), kind=kOutput, calls=%fused_computation.76.clone.1 | convolution fusion | flops 339477120 | bytes 1021952 | tf_op jit(solution)/shard_map/while/body/eval_jaxpr/sub | solution.py:62
  98.9 3.0 %fusion.130 = bf16[8,128,8,128]{1,3,2,0:T(8,128)(2,1)} fusion(bf16[8,128,8,128]{1,3,2,0:T(8,128)(2,1)} %get-tuple-element.208, s32[]{:T(128)} %get-tuple-element.207, f32[128,8]{0,1:T(8,128)S(1)} %select_bitcast_fusion.2, pred[128]{0:T(512)(128)(4,1)S(1)} %get-tuple-element.222, bf16[8,640,128]{1,2,0:T(8,128)(2,1)} %get-tuple-element.223, ...), kind=kOutput, calls=%fused_computation.18.clone.1 | convolution fusion | flops 507643520 | bytes 1449472 | tf_op jit(solution)/shard_map/while/body/eval_jaxpr/gqk,kd->qgd/dot_general | solution.py:64
  102.6 2.1 %fusion.129 = f32[8,128]{1,0:T(8,128)S(1)} fusion(pred[128,640]{0,1:T(8,128)(4,1)S(1)} %and_and_fusion.2, bf16[8,128,8,128]{3,1,2,0:T(8,128)(2,1)S(1)} %get-tuple-element.225, s32[]{:T(128)} %get-tuple-element.207, bf16[8,640,128]{2,1,0:T(8,128)(2,1)} %get-tuple-element.224), kind=kOutput, calls=%fused_computation.76.clone.1 | convolution fusion | flops 339477120 | bytes 1021952 | tf_op jit(solution)/shard_map/while/body/eval_jaxpr/sub | solution.py:62
  104.7 3.0 %fusion.130 = bf16[8,128,8,128]{1,3,2,0:T(8,128)(2,1)} fusion(bf16[8,128,8,128]{1,3,2,0:T(8,128)(2,1)} %get-tuple-element.208, s32[]{:T(128)} %get-tuple-element.207, f32[128,8]{0,1:T(8,128)S(1)} %select_bitcast_fusion.2, pred[128]{0:T(512)(128)(4,1)S(1)} %get-tuple-element.222, bf16[8,640,128]{1,2,0:T(8,128)(2,1)} %get-tuple-element.223, ...), kind=kOutput, calls=%fused_computation.18.clone.1 | convolution fusion | flops 507643520 | bytes 1449472 | tf_op jit(solution)/shard_map/while/body/eval_jaxpr/gqk,kd->qgd/dot_general | solution.py:64
  107.7 4.1 %copy.31 = bf16[128,8,8,128]{3,2,1,0:T(8,128)(2,1)} copy(bf16[128,8,8,128]{0,3,2,1:T(8,128)(2,1)} %bitcast.144) | data formatting | bytes 4194304 | tf_op jit(solution)/shard_map/transpose | solution.py:75
  (59 shorter events, 25.4 us)
Async XLA Ops:
  1.2 41.2 %collective-permute-start = (bf16[128,8,128]{0,2,1:T(8,128)(2,1)S(1)}, bf16[128,8,128]{0,2,1:T(8,128)(2,1)}, u32[]{:S(2)}, u32[]{:S(2)}) collective-permute-start(bf16[128,8,128]{0,2,1:T(8,128)(2,1)S(1)} %copy.20), channel_id=1, source_target_pairs={{0,4},{1,5},{2,6},{3,7},{8,12},{9,13},{10,14},{11,15},{16,20},{17,... | collective-permute-start | bytes 786440 | tf_op jit(solution)/shard_map/ppermute | solution.py:14
  5.8 40.5 %collective-permute-start.1 = (bf16[128,8,128]{0,2,1:T(8,128)(2,1)S(1)}, bf16[128,8,128]{0,2,1:T(8,128)(2,1)}, u32[]{:S(2)}, u32[]{:S(2)}) collective-permute-start(bf16[128,8,128]{0,2,1:T(8,128)(2,1)S(1)} %copy.20), channel_id=1, source_target_pairs={{0,3},{1,4},{2,5},{3,6},{4,7},{8,11},{9,12},{10,13},{11,14},{12,15... | collective-permute-start | bytes 786440 | tf_op jit(solution)/shard_map/ppermute | solution.py:14
  7.8 43.2 %collective-permute-start.2 = (bf16[128,8,128]{0,2,1:T(8,128)(2,1)S(1)}, bf16[128,8,128]{0,2,1:T(8,128)(2,1)S(1)}, u32[]{:S(2)}, u32[]{:S(2)}) collective-permute-start(bf16[128,8,128]{0,2,1:T(8,128)(2,1)S(1)} %copy.20), channel_id=1, source_target_pairs={{0,2},{1,3},{2,4},{3,5},{4,6},{5,7},{8,10},{9,11},{10,12},{11,13},... | collective-permute-start | bytes 786440 | tf_op jit(solution)/shard_map/ppermute | solution.py:14
  10.9 43.6 %collective-permute-start.3 = (bf16[128,8,128]{0,2,1:T(8,128)(2,1)S(1)}, bf16[128,8,128]{0,2,1:T(8,128)(2,1)S(1)}, u32[]{:S(2)}, u32[]{:S(2)}) collective-permute-start(bf16[128,8,128]{0,2,1:T(8,128)(2,1)S(1)} %copy.20), channel_id=1, source_target_pairs={{0,1},{1,2},{2,3},{3,4},{4,5},{5,6},{6,7},{8,9},{9,10},{10,11},{11... | collective-permute-start | bytes 786440 | tf_op jit(solution)/shard_map/ppermute | solution.py:14
  14.7 40.0 %collective-permute-start.4 = (bf16[128,8,128]{2,0,1:T(8,128)(2,1)S(1)}, bf16[128,8,128]{2,0,1:T(8,128)(2,1)S(1)}, u32[]{:S(2)}, u32[]{:S(2)}) collective-permute-start(bf16[128,8,128]{2,0,1:T(8,128)(2,1)S(1)} %copy.25), channel_id=1, source_target_pairs={{0,4},{1,5},{2,6},{3,7},{8,12},{9,13},{10,14},{11,15},{16,20},{17,... | collective-permute-start | bytes 786440 | tf_op jit(solution)/shard_map/ppermute | solution.py:14
  42.4 17.5 %collective-permute-start.5 = (bf16[128,8,128]{2,0,1:T(8,128)(2,1)S(1)}, bf16[128,8,128]{2,0,1:T(8,128)(2,1)S(1)}, u32[]{:S(2)}, u32[]{:S(2)}) collective-permute-start(bf16[128,8,128]{2,0,1:T(8,128)(2,1)S(1)} %copy.25), channel_id=1, source_target_pairs={{0,3},{1,4},{2,5},{3,6},{4,7},{8,11},{9,12},{10,13},{11,14},{12,15... | collective-permute-start | bytes 786440 | tf_op jit(solution)/shard_map/ppermute | solution.py:14
  46.3 13.7 %copy-start = (bf16[128,8,128]{2,1,0:T(8,128)(2,1)S(1)}, bf16[128,8,128]{2,1,0:T(8,128)(2,1)}, u32[]{:S(2)}) copy-start(bf16[128,8,128]{2,1,0:T(8,128)(2,1)} %param.10) | copy-start | bytes 786436
  46.4 13.5 %collective-permute-start.6 = (bf16[128,8,128]{2,0,1:T(8,128)(2,1)S(1)}, bf16[128,8,128]{2,0,1:T(8,128)(2,1)S(1)}, u32[]{:S(2)}, u32[]{:S(2)}) collective-permute-start(bf16[128,8,128]{2,0,1:T(8,128)(2,1)S(1)} %copy.25), channel_id=1, source_target_pairs={{0,2},{1,3},{2,4},{3,5},{4,6},{5,7},{8,10},{9,11},{10,12},{11,13},... | collective-permute-start | bytes 786440 | tf_op jit(solution)/shard_map/ppermute | solution.py:14
  51.0 8.9 %collective-permute-start.7 = (bf16[128,8,128]{2,0,1:T(8,128)(2,1)S(1)}, bf16[128,8,128]{2,0,1:T(8,128)(2,1)S(1)}, u32[]{:S(2)}, u32[]{:S(2)}) collective-permute-start(bf16[128,8,128]{2,0,1:T(8,128)(2,1)S(1)} %copy.25), channel_id=1, source_target_pairs={{0,1},{1,2},{2,3},{3,4},{4,5},{5,6},{6,7},{8,9},{9,10},{10,11},{11... | collective-permute-start | bytes 786440 | tf_op jit(solution)/shard_map/ppermute | solution.py:14
  54.7 5.4 %copy-start.1 = (bf16[640,8,128]{0,2,1:T(8,128)(2,1)}, bf16[640,8,128]{0,2,1:T(8,128)(2,1)S(1)}, u32[]{:S(2)}) copy-start(bf16[640,8,128]{0,2,1:T(8,128)(2,1)S(1)} %constant_dynamic-update-slice_fusion) | copy-start | bytes 3932164
  60.1 1.1 copy-start.2
where the time goes:
time: 113 us; the launch traced here: 112 us
  matrix products  40.8 us (36%)
  starting transfers between devices  23.8 us (21%)
  blocking collectives  16.1 us (14%)
  local copies, waits for them, and re-layouts  14.5 us (13%)
  other arithmetic  10.9 us (10%)
  waiting for transfers between devices  5.15 us (5%)
    dot_general x8, matrix products, one_group(): jnp.einsum('gqk,kd->qgd', weights.astype(jnp.bfloat16), value_group, pref...  24.2 us
    ppermute x8, starting transfers between devices, from_behind(): return lax.ppermute(array, axis, pairs)  23.8 us
    sub x8, matrix products, one_group(): weights = jnp.where(allowed[None], jnp.exp(scores - top), 0.0)  16.7 us
    all_gather x1, blocking collectives, local(): all_docs = lax.all_gather(doc_ids, 'seq', axis=0, tiled=True)  16.1 us
    unnamed x17, local copies, waits for them, and re-layouts  8.41 us
    and x8, other arithmetic, window_attend(): (key_doc[None, :] == query_doc[:, None]) & (key_pos[None, :] <= query_pos...  5.48 us
    ppermute x8, waiting for transfers between devices, from_behind(): return lax.ppermute(array, axis, pairs)  5.15 us
    gather x2, other arithmetic, local(): jnp.repeat(counts, shard_rows, total_repeat_length=row_count)  4.65 us
  transfers between devices with their start and end apart: 8, of which 1 were waited for; matrix products, arithmetic and copies ran while one was open for 12% of the time, Pallas kernels for 0%

commit v1 on v0

v1 whole, which is shorter than its diff:
```python
import functools
import math

import jax
import jax.numpy as jnp
from jax import lax
from jax.experimental import pallas as pl
from jax.experimental.pallas import tpu as pltpu
from jax.sharding import PartitionSpec as P

DOC_MOST = 512
MESH = pl.DeviceIdType.MESH
NEG = -1e30


def kernel(
    n, reach, tile,
    counts_ref, q_hbm, kv_hbm, doc_row_ref, doc_col_ref, out_hbm,
    win, q_vmem, o_vmem, dwin, bias,
    own_sem, q_sem, o_sem, send_sem, recv_sem, dsend_sem, drecv_sem,
):
    me = lax.axis_index("seq")
    heads, shard_rows, group, width = q_vmem.shape
    blocks = reach + 1
    keys_all = blocks * shard_rows
    rows = shard_rows * group
    tree = n == 8 and reach == 4

    def own_copy(h):
        return pltpu.make_async_copy(kv_hbm.at[h], win.at[h, :, reach], own_sem.at[h])

    def q_copy(h):
        return pltpu.make_async_copy(q_hbm.at[:, h], q_vmem.at[h], q_sem.at[h])

    def o_copy(h):
        return pltpu.make_async_copy(o_vmem.at[h], out_hbm.at[:, h], o_sem.at[h])

    def send(h, kind, from_off, to, to_off):
        return pltpu.make_async_remote_copy(
            src_ref=win.at[h, :, reach - from_off],
            dst_ref=win.at[h, :, reach - to_off],
            send_sem=send_sem.at[h, kind],
            recv_sem=recv_sem.at[h, to_off - 1],
            device_id={"seq": to},
            device_id_type=MESH,
        )

    def send_docs(off):
        return pltpu.make_async_remote_copy(
            src_ref=doc_row_ref,
            dst_ref=dwin.at[reach - off],
            send_sem=dsend_sem.at[off - 1],
            recv_sem=drecv_sem.at[off - 1],
            device_id={"seq": lax.rem(me + off, n)},
            device_id_type=MESH,
        )

    def wait_block(h, off):
        send(h, 0, 0, lax.rem(me + 1, n), off).wait_recv()

    def loop(body, count=None):
        lax.fori_loop(0, heads if count is None else count, lambda i, c: (body(i), c)[1], 0)

    loop(lambda h: own_copy(h).start())
    loop(lambda h: q_copy(h).start())

    barrier = pltpu.get_barrier_semaphore()
    for step in range(1, n):
        pl.semaphore_signal(
            barrier, inc=1, device_id={"seq": lax.rem(me + step, n)}, device_id_type=MESH
        )
    pl.semaphore_wait(barrier, n - 1)

    even = lax.rem(me, 2) == 0
    chip_odd = lax.rem(me // 2, 2) == 1
    if tree:
        own_sends = [
            (0, jnp.logical_not(chip_odd), 2),
            (1, me < 4, 4),
            (2, even, 1),
        ]
    else:
        own_sends = [(off - 1, me + off < n, off) for off in range(1, reach + 1)]

    for off in range(1, reach + 1):
        @pl.when(me + off < n)
        def _(off=off):
            send_docs(off).start()

    def start_own(h):
        own_copy(h).wait()
        for kind, cond, off in own_sends:
            @pl.when(cond)
            def _(kind=kind, off=off):
                send(h, kind, 0, lax.rem(me + off, n), off).start()

    loop(start_own)

    for off in range(1, reach + 1):
        @pl.when(me < off)
        def _(off=off):
            dwin[reach - off] = jnp.full(dwin.shape[1:], -1, jnp.int32)

            def clear(h):
                win[h, :, reach - off] = jnp.zeros((2, shard_rows, width), win.dtype)

            loop(clear)

    for off in range(1, reach + 1):
        @pl.when(me >= off)
        def _(off=off):
            send_docs(off).wait_recv()

    lane = lax.broadcasted_iota(jnp.int32, (shard_rows, shard_rows), 1)
    row = lax.broadcasted_iota(jnp.int32, (shard_rows, shard_rows), 0)
    for slot in range(blocks):
        off = reach - slot
        count = counts_ref[lax.max(me - off, 0)]
        docs = doc_row_ref[0:1, :] if off == 0 else dwin[slot, 0:1, :]
        allowed = (docs == doc_col_ref[...]) & (lane < count)
        if off == 0:
            allowed = allowed & (lane <= row)
        part = jnp.where(allowed, 0.0, NEG).astype(jnp.float32)
        part = jnp.broadcast_to(part[:, None, :], (shard_rows, group, shard_rows))
        bias[:, slot * shard_rows : (slot + 1) * shard_rows] = part.reshape(rows, shard_rows)

    own_count = counts_ref[me]
    factor = math.log2(math.e) / math.sqrt(width)

    def partner():
        return me + 1 - 2 * lax.rem(me, 2)

    def relay_two(h):
        wait_block(h, 2)

        @pl.when(even)
        def _():
            send(h, 3, 2, partner(), 3).start()

        @pl.when(jnp.logical_not(even))
        def _():
            send(h, 3, 2, partner(), 1).start()

    def stage_a(h):
        @pl.when(me >= 4)
        def _():
            wait_block(h, 4)

            @pl.when(me >= 6)
            def _():
                send(h, 5, 4, me - 2, 2).start()

            @pl.when(jnp.logical_not(even))
            def _():
                send(h, 4, 4, me - 1, 3).start()

        @pl.when(chip_odd)
        def _():
            relay_two(h)

    def is_b():
        return (me == 4) | (me == 5)

    def attend(h):
        q_copy(h).wait()
        keys = win[h, 0].reshape(keys_all, width)
        values = win[h, 1].reshape(keys_all, width)
        for start in range(0, rows, tile):
            pos = slice(start // group, (start + tile) // group)
            q = q_vmem[h, pos].reshape(tile, width)
            s = lax.dot_general(
                q, keys, (((1,), (1,)), ((), ())), preferred_element_type=jnp.float32
            )
            x = s * factor + bias[start : start + tile, :]
            top = jnp.max(x, axis=-1, keepdims=True)
            p = jnp.exp2(x - top)
            norm = jnp.sum(p, axis=-1, keepdims=True)
            o = lax.dot_general(
                p.astype(jnp.bfloat16), values, (((1,), (0,)), ((), ())),
                preferred_element_type=jnp.float32,
            )
            r = lax.broadcasted_iota(jnp.int32, (tile, width), 0) + start
            live = r < own_count * group
            o = jnp.where(live, o / norm, 0.0).astype(jnp.bfloat16)
            o_vmem[h, pos] = o.reshape(tile // group, group, width)
        o_copy(h).start()

    def step(it):
        if tree:
            @pl.when(it < heads)
            def _():
                stage_a(it)

            @pl.when((it >= 1) & (it < heads + 1) & is_b())
            def _():
                relay_two(it - 1)

            @pl.when(it >= 2)
            def _():
                for off in (1, 3):
                    @pl.when(me >= off)
                    def _(off=off):
                        wait_block(it - 2, off)
                attend(it - 2)
        else:
            for off in range(1, reach + 1):
                @pl.when(me >= off)
                def _(off=off):
                    wait_block(it, off)
            attend(it)

    loop(step, heads + 2 if tree else heads)

    def finish(h):
        o_copy(h).wait()
        for kind, cond, off in own_sends:
            @pl.when(cond)
            def _(kind=kind, off=off):
                send(h, kind, 0, lax.rem(me + off, n), off).wait_send()
        if tree:
            @pl.when(me >= 2)
            def _():
                send(h, 3, 2, partner(), 1).wait_send()

            @pl.when((me >= 4) & jnp.logical_not(even))
            def _():
                send(h, 4, 4, me - 1, 3).wait_send()

            @pl.when(me >= 6)
            def _():
                send(h, 5, 4, me - 2, 2).wait_send()

    loop(finish)
    for off in range(1, reach + 1):
        @pl.when(me + off < n)
        def _(off=off):
            send_docs(off).wait_send()


def local(n, queries, keys, values, doc_ids, counts):
    shard_rows, q_heads, width = queries.shape
    heads = keys.shape[1]
    group = q_heads // heads
    reach = min((DOC_MOST + shard_rows - 1) // shard_rows, n - 1)
    rows = shard_rows * group
    kv = jnp.stack([jnp.transpose(keys, (1, 0, 2)), jnp.transpose(values, (1, 0, 2))], axis=1)
    doc_row = jnp.broadcast_to(doc_ids[None, :], (8, shard_rows))
    doc_col = jnp.broadcast_to(doc_ids[:, None], (shard_rows, shard_rows))
    out = pl.pallas_call(
        functools.partial(kernel, n, reach, 128),
        out_shape=jax.ShapeDtypeStruct((shard_rows, heads, group, width), jnp.bfloat16),
        in_specs=[
            pl.BlockSpec(memory_space=pltpu.SMEM),
            pl.BlockSpec(memory_space=pl.ANY),
            pl.BlockSpec(memory_space=pl.ANY),
            pl.BlockSpec(memory_space=pltpu.VMEM),
            pl.BlockSpec(memory_space=pltpu.VMEM),
        ],
        out_specs=pl.BlockSpec(memory_space=pl.ANY),
        scratch_shapes=[
            pltpu.VMEM((heads, 2, reach + 1, shard_rows, width), jnp.bfloat16),
            pltpu.VMEM((heads, shard_rows, group, width), jnp.bfloat16),
            pltpu.VMEM((heads, shard_rows, group, width), jnp.bfloat16),
            pltpu.VMEM((reach, 8, shard_rows), jnp.int32),
            pltpu.VMEM((rows, (reach + 1) * shard_rows), jnp.float32),
            pltpu.SemaphoreType.DMA((heads,)),
            pltpu.SemaphoreType.DMA((heads,)),
            pltpu.SemaphoreType.DMA((heads,)),
            pltpu.SemaphoreType.DMA((heads, 6)),
            pltpu.SemaphoreType.DMA((heads, reach)),
            pltpu.SemaphoreType.DMA((reach,)),
            pltpu.SemaphoreType.DMA((reach,)),
        ],
        compiler_params=pltpu.CompilerParams(collective_id=0, has_side_effects=True),
    )(counts, queries.reshape(shard_rows, heads, group, width), kv, doc_row, doc_col)
    return out.reshape(shard_rows, q_heads, width)


def solution(mesh):
    in_specs = (
        P(("dp", "seq"), None, None),
        P(("dp", "seq"), None, None),
        P(("dp", "seq"), None, None),
        P(("dp", "seq")),
        P("dp"),
    )
    out_specs = P(("dp", "seq"), None, None)
    return jax.shard_map(
        functools.partial(local, mesh.shape["seq"]),
        mesh=mesh, in_specs=in_specs, out_specs=out_specs, check_vma=False,
    )
```

time: 113 us -> 42.7 us (0.38)
  the two profiles are of different devices: /device:TPU:1 before, /device:TPU:29 now
where the time goes in v1:
time: 42.7 us; the launch traced here: 42.5 us
  Pallas kernels  34.8 us (81%)
  local copies, waits for them, and re-layouts  6.81 us (16%)
  other arithmetic  0.84 us (2%)
    pallas_call x1, Pallas kernels, local(): pl.pallas_call(functools.partial(kernel, n, reach, 128), out_shape=jax.Sh...  34.8 us
    unnamed x1, local copies, waits for them, and re-layouts  3.08 us
    broadcast_in_dim x1, local copies, waits for them, and re-layouts, local(): doc_col = jnp.broadcast_to(doc_ids[:, None], (shard_rows, shard_rows))  1.37 us
    broadcast_in_dim x1, local copies, waits for them, and re-layouts, local(): doc_row = jnp.broadcast_to(doc_ids[None, :], (8, shard_rows))  1.24 us
    another operation x1, local copies, waits for them, and re-layouts, local(): jnp.stack([jnp.transpose(keys, (1, 0, 2)), jnp.transpose(values, (1, 0, 2...  1.12 us

profile of v1, /device:TPU:29, one launch (start us, length us, event | category | flops | bytes accessed | tf_op | source)
XLA Modules:
  0.0 42.5 jit_solution(3849000863783533967)
XLA Ops:
  0.0 1.2 %broadcast_in_dim.4.doc_row_ref = s32[8,128]{1,0:T(8,128)} broadcast(s32[128]{0:T(128)} %param.8), dimensions={1} | broadcast | bytes 4608 | tf_op jit(solution)/shard_map/broadcast_in_dim | solution.py:247
  1.2 1.4 %broadcast_in_dim.5.doc_col_ref = s32[128,128]{1,0:T(8,128)} broadcast(s32[128]{0:T(128)} %param.8), dimensions={0} | broadcast | bytes 66048 | tf_op jit(solution)/shard_map/broadcast_in_dim | solution.py:248
  2.6 1.1 %copy_bitcast_fusion = (bf16[8,1,128,128]{3,2,1,0:T(8,128)(2,1)S(1)}, bf16[8,1,128,128]{3,2,1,0:T(8,128)(2,1)S(1)}) fusion(bf16[128,8,128]{2,1,0:T(8,128)(2,1)} %param.7, bf16[128,8,128]{2,1,0:T(8,128)(2,1)} %param.6), kind=kLoop, calls=%fused_computation.1 | loop fusion | bytes 1048576 | tf_op jit(solution)/shard_map/stack | solution.py:246
  3.7 0.8 %pad_maximum_fusion.kv_hbm = bf16[8,2,128,128]{3,2,1,0:T(8,128)(2,1)} fusion(bf16[8,1,128,128]{3,2,1,0:T(8,128)(2,1)S(1)} %get-tuple-element.5, bf16[8,1,128,128]{3,2,1,0:T(8,128)(2,1)S(1)} %get-tuple-element.6), kind=kLoop, calls=%fused_computation | loop fusion | flops 262144 | bytes 1048576 | tf_op jit(solution)/shard_map/stack | solution.py:246
  4.6 34.8 %shard_map.55 = bf16[128,8,8,128]{3,2,1,0:T(8,128)(2,1)} custom-call(s32[8]{0:T(128)} %counts_ref.1, bf16[128,8,8,128]{3,2,1,0:T(8,128)(2,1)} %bitcast.11, bf16[8,2,128,128]{3,2,1,0:T(8,128)(2,1)} %pad_maximum_fusion.kv_hbm, s32[8,128]{1,0:T(8,128)} %broadcast_in_dim.4.doc_row_ref, s32[128,128]{1,0:T(8,128)} %broadcast_in_dim.5.doc_col_ref), custom_call_target="tpu_custom_call" | custom-call | tf_op jit(solution)/shard_map/pallas_call | solution.py:249
  39.4 3.1 %copy.11 = bf16[128,64,128]{2,1,0:T(8,128)(2,1)} copy(bf16[128,64,128]{2,1,0:T(8,128)(2,1)} %bitcast.10) | data formatting | bytes 4194304

commit v2 on v1

v2 whole, which is shorter than its diff:
```python
import functools
import math

import jax
import jax.numpy as jnp
from jax import lax
from jax.experimental import pallas as pl
from jax.experimental.pallas import tpu as pltpu
from jax.sharding import PartitionSpec as P

DOC_MOST = 512
MESH = pl.DeviceIdType.MESH
NEG = -1e30


def kernel(
    n, reach, tile,
    counts_hbm, q_hbm, k_ref, v_ref, docs_hbm, out_ref,
    win, q_vmem, dwin, bias, counts_ref, small_sem,
    q_sem, send_sem, recv_sem, dsend_sem, drecv_sem,
):
    me = lax.axis_index("seq")
    heads, shard_rows, group, width = q_vmem.shape
    blocks = reach + 1
    keys_all = blocks * shard_rows
    rows = shard_rows * group
    tree = n == 8 and reach == 4

    def q_copy(h):
        return pltpu.make_async_copy(q_hbm.at[:, h], q_vmem.at[h], q_sem.at[h])

    def send(h, part, kind, from_off, to, to_off):
        source = (k_ref, v_ref)[part].at[h] if from_off == 0 else win.at[h, part, reach - from_off]
        return pltpu.make_async_remote_copy(
            src_ref=source,
            dst_ref=win.at[h, part, reach - to_off],
            send_sem=send_sem.at[h, part, kind],
            recv_sem=recv_sem.at[h, part, to_off - 1],
            device_id={"seq": to},
            device_id_type=MESH,
        )

    def send_docs(off):
        return pltpu.make_async_remote_copy(
            src_ref=dwin.at[reach],
            dst_ref=dwin.at[reach - off],
            send_sem=dsend_sem.at[off - 1],
            recv_sem=drecv_sem.at[off - 1],
            device_id={"seq": lax.rem(me + off, n)},
            device_id_type=MESH,
        )

    def wait_block(h, part, off):
        send(h, part, 0, 0, lax.rem(me + 1, n), off).wait_recv()

    def loop(body, count=None):
        lax.fori_loop(0, heads if count is None else count, lambda i, c: (body(i), c)[1], 0)

    doc_copy = pltpu.make_async_copy(docs_hbm, dwin.at[reach], small_sem.at[0])
    count_copy = pltpu.make_async_copy(counts_hbm, counts_ref, small_sem.at[1])
    doc_copy.start()
    count_copy.start()
    loop(lambda h: q_copy(h).start())

    barrier = pltpu.get_barrier_semaphore()
    for step in range(1, n):
        pl.semaphore_signal(
            barrier, inc=1, device_id={"seq": lax.rem(me + step, n)}, device_id_type=MESH
        )
    pl.semaphore_wait(barrier, n - 1)

    even = lax.rem(me, 2) == 0
    chip_odd = lax.rem(me // 2, 2) == 1
    if tree:
        own_sends = [
            (0, jnp.logical_not(chip_odd), 2),
            (1, me < 4, 4),
            (2, even, 1),
        ]
    else:
        own_sends = [(off - 1, me + off < n, off) for off in range(1, reach + 1)]

    def start_own(h):
        for kind, cond, off in own_sends:
            @pl.when(cond)
            def _(kind=kind, off=off):
                for part in range(2):
                    send(h, part, kind, 0, lax.rem(me + off, n), off).start()

    doc_copy.wait()
    count_copy.wait()
    for off in range(1, reach + 1):
        @pl.when(me + off < n)
        def _(off=off):
            send_docs(off).start()

    loop(start_own)

    def keep_own(h):
        win[h, 0, reach] = k_ref[h]
        win[h, 1, reach] = v_ref[h]

    loop(keep_own)

    for off in range(1, reach + 1):
        @pl.when(me < off)
        def _(off=off):
            dwin[reach - off] = jnp.full(dwin.shape[1:], -1, jnp.int32)

            def clear(h):
                win[h, :, reach - off] = jnp.zeros((2, shard_rows, width), win.dtype)

            loop(clear)

    for off in range(1, reach + 1):
        @pl.when(me >= off)
        def _(off=off):
            send_docs(off).wait_recv()

    lane = lax.broadcasted_iota(jnp.int32, (shard_rows, shard_rows), 1)
    row = lax.broadcasted_iota(jnp.int32, (shard_rows, shard_rows), 0)
    doc_col = jnp.transpose(jnp.broadcast_to(dwin[reach], (shard_rows, shard_rows)))
    for slot in range(blocks):
        off = reach - slot
        count = counts_ref[lax.max(me - off, 0)]
        docs = dwin[slot]
        allowed = (docs == doc_col) & (lane < count)
        if off == 0:
            allowed = allowed & (lane <= row)
        part = jnp.where(allowed, 0.0, NEG).astype(jnp.float32)
        part = jnp.broadcast_to(part[:, None, :], (shard_rows, group, shard_rows))
        bias[:, slot * shard_rows : (slot + 1) * shard_rows] = part.reshape(rows, shard_rows)

    own_count = counts_ref[me]
    factor = math.log2(math.e) / math.sqrt(width)

    def partner():
        return me + 1 - 2 * lax.rem(me, 2)

    def relay_two(h, part):
        wait_block(h, part, 2)

        @pl.when(even)
        def _():
            send(h, part, 3, 2, partner(), 3).start()

        @pl.when(jnp.logical_not(even))
        def _():
            send(h, part, 3, 2, partner(), 1).start()

    def relay_four(h, part):
        wait_block(h, part, 4)

        @pl.when(me >= 6)
        def _():
            send(h, part, 5, 4, me - 2, 2).start()

        @pl.when(jnp.logical_not(even))
        def _():
            send(h, part, 4, 4, me - 1, 3).start()

    def relay(h):
        for part in range(2):
            @pl.when(me >= 4)
            def _(part=part):
                relay_four(h, part)

            @pl.when(me >= 2)
            def _(part=part):
                relay_two(h, part)

    def attend(h):
        q_copy(h).wait()
        keys = win[h, 0].reshape(keys_all, width)
        values = win[h, 1].reshape(keys_all, width)

        def scores(start):
            q = q_vmem[h, start // group : (start + tile) // group].reshape(tile, width)
            return lax.dot_general(
                q, keys, (((1,), (1,)), ((), ())), preferred_element_type=jnp.float32
            )

        s_next = scores(0)
        for start in range(0, rows, tile):
            s = s_next
            if start + tile < rows:
                s_next = scores(start + tile)
            x = s * factor + bias[start : start + tile, :]
            top = jnp.max(x, axis=-1, keepdims=True)
            p = jnp.exp2(x - top)
            norm = jnp.sum(p, axis=-1, keepdims=True)
            o = lax.dot_general(
                p.astype(jnp.bfloat16), values, (((1,), (0,)), ((), ())),
                preferred_element_type=jnp.float32,
            )
            r = lax.broadcasted_iota(jnp.int32, (tile, width), 0) + start
            o = jnp.where(r < own_count * group, o / norm, 0.0).astype(jnp.bfloat16)
            out_ref[start // group : (start + tile) // group, h] = o.reshape(
                tile // group, group, width
            )

    def arrivals(h, offs):
        for off in offs:
            @pl.when(me >= off)
            def _(off=off):
                for part in range(2):
                    wait_block(h, part, off)

    def step(it):
        if tree:
            @pl.when(it < heads)
            def _():
                relay(it)

            @pl.when(it >= 1)
            def _():
                arrivals(it - 1, (1, 3))
                attend(it - 1)
        else:
            arrivals(it, range(1, reach + 1))
            attend(it)

    loop(step, heads + 1 if tree else heads)

    def finish(h):
        for part in range(2):
            for kind, cond, off in own_sends:
                @pl.when(cond)
                def _(part=part, kind=kind, off=off):
                    send(h, part, kind, 0, lax.rem(me + off, n), off).wait_send()
            if tree:
                @pl.when(me >= 2)
                def _(part=part):
                    send(h, part, 3, 2, partner(), 1).wait_send()

                @pl.when((me >= 4) & jnp.logical_not(even))
                def _(part=part):
                    send(h, part, 4, 4, me - 1, 3).wait_send()

                @pl.when(me >= 6)
                def _(part=part):
                    send(h, part, 5, 4, me - 2, 2).wait_send()

    loop(finish)
    for off in range(1, reach + 1):
        @pl.when(me + off < n)
        def _(off=off):
            send_docs(off).wait_send()


def local(n, queries, keys, values, doc_ids, counts):
    shard_rows, q_heads, width = queries.shape
    heads = keys.shape[1]
    group = q_heads // heads
    reach = min((DOC_MOST + shard_rows - 1) // shard_rows, n - 1)
    rows = shard_rows * group
    out = pl.pallas_call(
        functools.partial(kernel, n, reach, 256),
        out_shape=jax.ShapeDtypeStruct((shard_rows, heads, group, width), jnp.bfloat16),
        in_specs=[
            pl.BlockSpec(memory_space=pltpu.HBM),
            pl.BlockSpec(memory_space=pltpu.HBM),
            pl.BlockSpec(memory_space=pltpu.VMEM),
            pl.BlockSpec(memory_space=pltpu.VMEM),
            pl.BlockSpec(memory_space=pltpu.HBM),
        ],
        out_specs=pl.BlockSpec(memory_space=pltpu.VMEM),
        scratch_shapes=[
            pltpu.VMEM((heads, 2, reach + 1, shard_rows, width), jnp.bfloat16),
            pltpu.VMEM((heads, shard_rows, group, width), jnp.bfloat16),
            pltpu.VMEM((reach + 1, 1, shard_rows), jnp.int32),
            pltpu.VMEM((rows, (reach + 1) * shard_rows), jnp.float32),
            pltpu.SMEM(counts.shape, jnp.int32),
            pltpu.SemaphoreType.DMA((2,)),
            pltpu.SemaphoreType.DMA((heads,)),
            pltpu.SemaphoreType.DMA((heads, 2, 6)),
            pltpu.SemaphoreType.DMA((heads, 2, reach)),
            pltpu.SemaphoreType.DMA((reach,)),
            pltpu.SemaphoreType.DMA((reach,)),
        ],
        compiler_params=pltpu.CompilerParams(
            collective_id=0, has_side_effects=True, vmem_limit_bytes=51 << 20
        ),
    )(
        counts,
        queries.reshape(shard_rows, heads, group, width),
        jnp.transpose(keys, (1, 0, 2)),
        jnp.transpose(values, (1, 0, 2)),
        doc_ids.reshape(1, shard_rows),
    )
    return out.reshape(shard_rows, q_heads, width)


def solution(mesh):
    in_specs = (
        P(("dp", "seq"), None, None),
        P(("dp", "seq"), None, None),
        P(("dp", "seq"), None, None),
        P(("dp", "seq")),
        P("dp"),
    )
    out_specs = P(("dp", "seq"), None, None)
    return jax.shard_map(
        functools.partial(local, mesh.shape["seq"]),
        mesh=mesh, in_specs=in_specs, out_specs=out_specs, check_vma=False,
    )
```

time: 42.7 us -> 26.9 us (0.63)
  Pallas kernels: 34.8 us -> 23 us
  local copies, waits for them, and re-layouts: 6.81 us -> 3.75 us
  other arithmetic: 0.84 us -> 0 us
    pallas_call x1, Pallas kernels: 34.8 us -> 23 us  [local(): pl.pallas_call(functools.partial(kernel, n, reach, 256), out_shape=jax.Sh...]
    broadcast_in_dim x2 -> x0, local copies, waits for them, and re-layouts: 2.61 us -> none  [the longest x1 1.37 us: local(): doc_col = jnp.broadcast_to(doc_ids[:, None], (shard_rows, shard_rows))]
    transpose x0 -> x1, local copies, waits for them, and re-layouts: none -> 1.12 us  [local(): jnp.transpose(values, (1, 0, 2))]
    another operation x1 -> x0, local copies, waits for them, and re-layouts: 1.12 us -> none  [local(): jnp.stack([jnp.transpose(keys, (1, 0, 2)), jnp.transpose(values, (1, 0, 2...]
    another operation x1 -> x0, other arithmetic: 0.84 us -> none  [local(): jnp.stack([jnp.transpose(keys, (1, 0, 2)), jnp.transpose(values, (1, 0, 2...]
    unnamed x1 -> x5, local copies, waits for them, and re-layouts: 3.08 us -> 2.63 us
where the time goes in v2:
time: 26.9 us; the launch traced here: 26.8 us
  Pallas kernels  23 us (86%)
  local copies, waits for them, and re-layouts  3.75 us (14%)
    pallas_call x1, Pallas kernels, local(): pl.pallas_call(functools.partial(kernel, n, reach, 256), out_shape=jax.Sh...  23 us
    unnamed x5, local copies, waits for them, and re-layouts  2.63 us
    transpose x1, local copies, waits for them, and re-layouts, local(): jnp.transpose(values, (1, 0, 2))  1.12 us

profile of v2, /device:TPU:29, one launch (start us, length us, event | category | flops | bytes accessed | tf_op | source)
XLA Modules:
  0.0 26.8 jit_solution(12404693588752868677)
XLA Ops:
  0.0 1.1 %copy_bitcast_fusion = (bf16[8,128,128]{2,1,0:T(8,128)(2,1)S(1)}, bf16[8,128,128]{2,1,0:T(8,128)(2,1)S(1)}) fusion(bf16[128,8,128]{2,1,0:T(8,128)(2,1)} %param.7, bf16[128,8,128]{2,1,0:T(8,128)(2,1)} %param.6), kind=kLoop, calls=%fused_computation | loop fusion | bytes 1048576 | tf_op jit(solution)/shard_map/transpose | solution.py:288
  1.1 0.0 copy-start
  1.1 0.6 %copy-done = s32[8]{0:T(128)S(1)} copy-done((s32[8]{0:T(128)S(1)}, s32[8]{0:T(128)}, u32[]{:S(2)}) %copy-start) | copy-done | bytes 56
  1.8 0.0 copy-start.1
  1.8 0.7 %copy-done.1 = s32[128]{0:T(128)S(1)} copy-done((s32[128]{0:T(128)S(1)}, s32[128]{0:T(128)}, u32[]{:S(2)}) %copy-start.1) | copy-done | bytes 536
  2.4 23.0 %shard_map.55 = bf16[128,8,8,128]{3,2,1,0:T(8,128)(2,1)S(1)} custom-call(s32[8]{0:T(128)S(1)} %copy-done, bf16[128,8,8,128]{3,2,1,0:T(8,128)(2,1)} %bitcast.9, bf16[8,128,128]{2,1,0:T(8,128)(2,1)S(1)} %get-tuple-element.6.k_ref, bf16[8,128,128]{2,1,0:T(8,128)(2,1)S(1)} %get-tuple-element.5.v_ref, s32[1,128]{1,0:T(1,128)S(1)} %bitcast.8), custom_call_target="tpu_custom_call" | custom-call | tf_op jit(solution)/shard_map/pallas_call | solution.py:257
  25.4 1.3 %copy.11 = bf16[128,64,128]{2,1,0:T(8,128)(2,1)} copy(bf16[128,64,128]{2,1,0:T(8,128)(2,1)S(1)} %bitcast.7) | data formatting | bytes 4194304
Async XLA Ops:
  1.1 0.7 %copy-start = (s32[8]{0:T(128)S(1)}, s32[8]{0:T(128)}, u32[]{:S(2)}) copy-start(s32[8]{0:T(128)} %counts_hbm.1) | copy-start | bytes 100
  1.8 0.7 %copy-start.1 = (s32[128]{0:T(128)S(1)}, s32[128]{0:T(128)}, u32[]{:S(2)}) copy-start(s32[128]{0:T(128)} %param.8) | copy-start | bytes 1540
